TPU v7x, 32 devices: a whole 2x2x4 slice. The times are simulated.
32 devices in a mesh: row: 8 (over z, core), col: 4 (over y, x).
Axes of the slice: x: 2, y: 2, z: 4, core: 2. Of those that a mesh axis runs over, the one named last changes fastest.
Arguments:
- attn_out: bfloat16 [6, 512, 2048], P(None, 'col', 'row'), may hold values from -0.625 to 0.625
- out_cotangent: bfloat16 [6, 512, 2048], P(None, 'row', 'col'), may hold values from -6 to 6
- frozen: bfloat16 [6, 2048, 2048], P(None, 'row', 'col'), may hold values from -0.5 to 0.5
- adapt_in: bfloat16 [6, 32, 2048], P(None, None, 'row'), may hold values from -0.125 to 0.125
- adapt_out: bfloat16 [6, 32, 2048], P(None, None, 'col'), may hold values from -1 to 1
- magnitude: float32 [6, 2048], P(None, 'col'), may hold values from 0.1 to 1.9
Outputs:
- input_grad: bfloat16 [6, 512, 2048], P(None, 'col', 'row')
- adapt_in_grad: float32 [6, 32, 2048], P(None, None, 'row')
- adapt_out_grad: float32 [6, 32, 2048], P(None, None, 'col')
- magnitude_grad: float32 [6, 2048], P(None, 'col')
All inputs are finite; a program needn't handle non-finite values.
Results may differ from a plain program's by a relative error of at most 0.0065.
Values may be sent and summed in bfloat16 or wider, within the bound.
A program may use at most 64 MiB of HBM per device.

v0:
```python
import jax
import jax.numpy as jnp
from jax import lax
from jax.sharding import PartitionSpec as P

precise = lax.Precision.HIGHEST


def one_layer(acts, grads, frozen, adapt_in, adapt_out, magnitude):
    merged = frozen.astype(jnp.float32) + lax.dot_general(
        adapt_in, adapt_out, (((0,), (0,)), ((), ())), preferred_element_type=jnp.float32
    )
    squares_part = jnp.sum(merged * merged, axis=0)
    grads_all = lax.all_gather(grads, "row", axis=0, tiled=True)
    outer = lax.dot_general(
        lax.all_gather(acts, "col", axis=0, tiled=True),
        grads_all,
        (((0,), (0,)), ((), ())),
        preferred_element_type=jnp.float32,
    )
    dots_part = jnp.sum(merged * outer, axis=0)
    adapt_in_wide = adapt_in.astype(jnp.float32)
    inner_outer = jnp.dot(adapt_in_wide, outer, precision=precise)
    inner_merged = jnp.dot(adapt_in_wide, merged, precision=precise)
    squares, dots, inner_outer, inner_merged = lax.psum(
        (squares_part, dots_part, inner_outer, inner_merged), "row"
    )
    norms = jnp.sqrt(squares + 0.25)
    scales = magnitude / norms
    correct = -magnitude * dots / (norms * norms * norms)
    delta = outer * scales + merged * correct
    out_grad = inner_outer * scales + inner_merged * correct
    magnitude_grad = dots / norms
    in_part = lax.dot_general(
        adapt_out.astype(jnp.float32), delta, (((1,), (1,)), ((), ())), precision=precise
    )
    in_grad = lax.psum(in_part, "col")
    scaled = (grads_all * scales).astype(jnp.bfloat16)
    weight_low = merged.astype(jnp.bfloat16)
    summed = lax.psum_scatter(
        lax.dot_general(
            scaled, weight_low, (((1,), (1,)), ((), ())), preferred_element_type=jnp.float32
        ),
        "col",
        scatter_dimension=0,
        tiled=True,
    )
    return (summed.astype(jnp.bfloat16), in_grad, out_grad, magnitude_grad)


def body(attn_out, out_cotangent, frozen, adapt_in, adapt_out, magnitude):
    results = [
        one_layer(
            attn_out[layer_at],
            out_cotangent[layer_at],
            frozen[layer_at],
            adapt_in[layer_at],
            adapt_out[layer_at],
            magnitude[layer_at],
        )
        for layer_at in range(frozen.shape[0])
    ]
    return (
        jnp.stack([item[0] for item in results]),
        jnp.stack([item[1] for item in results]),
        jnp.stack([item[2] for item in results]),
        jnp.stack([item[3] for item in results]),
    )


def solution(mesh):
    return jax.shard_map(
        body,
        mesh=mesh,
        in_specs=(
            P(None, "col", "row"),
            P(None, "row", "col"),
            P(None, "row", "col"),
            P(None, None, "row"),
            P(None, None, "col"),
            P(None, "col"),
        ),
        out_specs=(
            P(None, "col", "row"),
            P(None, None, "row"),
            P(None, None, "col"),
            P(None, "col"),
        ),
        check_vma=False,
    )
```

profile of v0, /device:TPU:1, one launch (start us, length us, event | category | flops | bytes accessed | tf_op | source)
XLA Modules:
  0.0 472.5 jit_solution(1073232057520900545)
XLA Ops:
  7.2 1.1 fusion.151
  8.3 16.4 %all-gather = bf16[1,512,512]{2,1,0:T(8,128)(2,1)S(1)} all-gather(bf16[1,64,512]{2,1,0:T(8,128)(2,1)S(1)} %get-tuple-element.56), channel_id=2, replica_groups=mesh['row'=8,'col'=4] {'row'}, dimensions={1}, use_global_device_ids=true | all-gather | bytes 589824 | tf_op jit(solution)/shard_map/all_gather | solution.py:14
  24.7 7.0 %all-gather.6 = bf16[1,512,256]{2,1,0:T(8,128)(2,1)S(1)} all-gather(bf16[1,128,256]{2,1,0:T(8,128)(2,1)S(1)} %get-tuple-element.50), channel_id=8, replica_groups=mesh['row'=8,'col'=4] {'col'}, dimensions={1}, use_global_device_ids=true | all-gather | bytes 327680 | tf_op jit(solution)/shard_map/all_gather | solution.py:16
  31.6 17.0 %all-gather.1 = bf16[1,512,512]{2,1,0:T(8,128)(2,1)S(1)} all-gather(bf16[1,64,512]{2,1,0:T(8,128)(2,1)S(1)} %get-tuple-element.55), channel_id=3, replica_groups=mesh['row'=8,'col'=4] {'row'}, dimensions={1}, use_global_device_ids=true | all-gather | bytes 589824 | tf_op jit(solution)/shard_map/all_gather | solution.py:14
  48.7 7.1 %all-gather.7 = bf16[1,512,256]{2,1,0:T(8,128)(2,1)S(1)} all-gather(bf16[1,128,256]{2,1,0:T(8,128)(2,1)S(1)} %get-tuple-element.49), channel_id=9, replica_groups=mesh['row'=8,'col'=4] {'col'}, dimensions={1}, use_global_device_ids=true | all-gather | bytes 327680 | tf_op jit(solution)/shard_map/all_gather | solution.py:16
  57.1 16.9 %all-gather.2 = bf16[1,512,512]{2,1,0:T(8,128)(2,1)S(1)} all-gather(bf16[1,64,512]{2,1,0:T(8,128)(2,1)S(1)} %get-tuple-element.54), channel_id=4, replica_groups=mesh['row'=8,'col'=4] {'row'}, dimensions={1}, use_global_device_ids=true | all-gather | bytes 589824 | tf_op jit(solution)/shard_map/all_gather | solution.py:14
  74.0 6.0 %all-gather.8 = bf16[1,512,256]{2,1,0:T(8,128)(2,1)S(1)} all-gather(bf16[1,128,256]{2,1,0:T(8,128)(2,1)S(1)} %get-tuple-element.48), channel_id=10, replica_groups=mesh['row'=8,'col'=4] {'col'}, dimensions={1}, use_global_device_ids=true | all-gather | bytes 327680 | tf_op jit(solution)/shard_map/all_gather | solution.py:16
  80.6 17.0 %all-gather.3 = bf16[1,512,512]{2,1,0:T(8,128)(2,1)S(1)} all-gather(bf16[1,64,512]{2,1,0:T(8,128)(2,1)S(1)} %get-tuple-element.53), channel_id=5, replica_groups=mesh['row'=8,'col'=4] {'row'}, dimensions={1}, use_global_device_ids=true | all-gather | bytes 589824 | tf_op jit(solution)/shard_map/all_gather | solution.py:14
  97.6 6.9 %all-gather.9 = bf16[1,512,256]{2,1,0:T(8,128)(2,1)S(1)} all-gather(bf16[1,128,256]{2,1,0:T(8,128)(2,1)S(1)} %get-tuple-element.47), channel_id=11, replica_groups=mesh['row'=8,'col'=4] {'col'}, dimensions={1}, use_global_device_ids=true | all-gather | bytes 327680 | tf_op jit(solution)/shard_map/all_gather | solution.py:16
  105.1 16.8 %all-gather.4 = bf16[1,512,512]{2,1,0:T(8,128)(2,1)S(1)} all-gather(bf16[1,64,512]{2,1,0:T(8,128)(2,1)S(1)} %get-tuple-element.57), channel_id=6, replica_groups=mesh['row'=8,'col'=4] {'row'}, dimensions={1}, use_global_device_ids=true | all-gather | bytes 589824 | tf_op jit(solution)/shard_map/all_gather | solution.py:14
  122.0 6.1 %all-gather.10 = bf16[1,512,256]{2,1,0:T(8,128)(2,1)S(1)} all-gather(bf16[1,128,256]{2,1,0:T(8,128)(2,1)S(1)} %get-tuple-element.51), channel_id=12, replica_groups=mesh['row'=8,'col'=4] {'col'}, dimensions={1}, use_global_device_ids=true | all-gather | bytes 327680 | tf_op jit(solution)/shard_map/all_gather | solution.py:16
  128.7 17.0 %all-gather.5 = bf16[1,512,512]{2,1,0:T(8,128)(2,1)S(1)} all-gather(bf16[1,64,512]{2,1,0:T(8,128)(2,1)S(1)} %get-tuple-element.52), channel_id=7, replica_groups=mesh['row'=8,'col'=4] {'row'}, dimensions={1}, use_global_device_ids=true | all-gather | bytes 589824 | tf_op jit(solution)/shard_map/all_gather | solution.py:14
  145.7 7.1 %all-gather.11 = bf16[1,512,256]{2,1,0:T(8,128)(2,1)S(1)} all-gather(bf16[1,128,256]{2,1,0:T(8,128)(2,1)S(1)} %get-tuple-element.46), channel_id=13, replica_groups=mesh['row'=8,'col'=4] {'col'}, dimensions={1}, use_global_device_ids=true | all-gather | bytes 327680 | tf_op jit(solution)/shard_map/all_gather | solution.py:16
  153.1 0.8 copy-done.12
  154.2 25.1 %all-reduce = (f32[512]{0:T(512)}, f32[512]{0:T(512)}, f32[512]{0:T(512)S(1)}, f32[512]{0:T(512)S(1)}, f32[512]{0:T(512)S(1)}, /*index=5*/f32[512]{0:T(512)S(1)}...) all-reduce(f32[512]{0:T(512)S(1)} %get-tuple-element.15, ...), channel_id=1, replica_groups=mesh['row'=8,'col'=4] {'row'}, use_global_device_ids=true, to_apply=%region_1.0 | all-reduce | flops 6144 | bytes 49152 | tf_op jit(solution)/shard_map/psum | solution.py:25
  179.4 0.8 fusion.138
  180.2 2.1 convolution_bitcast_fusion.17
  182.4 2.1 convolution_bitcast_fusion.16
  184.5 1.0 convolution_bitcast_fusion.15
  185.6 1.0 convolution_bitcast_fusion.14
  186.7 1.0 convolution_bitcast_fusion.13
  187.7 1.0 convolution_bitcast_fusion.12
  189.0 0.9 convolution_bitcast_fusion.10
  189.9 2.0 convolution_bitcast_fusion.11
  191.9 0.9 convolution_bitcast_fusion.8
  192.9 0.9 convolution_bitcast_fusion.9
  193.8 0.9 convolution_bitcast_fusion.6
  194.7 0.9 convolution_bitcast_fusion.7
  195.6 0.9 convolution_bitcast_fusion.4
  196.6 0.9 convolution_bitcast_fusion.5
  197.5 0.9 convolution_bitcast_fusion.2
  198.4 0.9 convolution_bitcast_fusion.3
  199.4 0.9 convolution_bitcast_fusion
  200.3 0.9 convolution_bitcast_fusion.1
  201.3 2.2 fusion
  203.6 2.2 fusion.1
  205.9 1.2 fusion.2
  207.1 1.1 fusion.3
  208.4 1.1 fusion.4
  209.6 1.1 fusion.5
  211.4 22.4 %all-reduce.8.cloned.1.call-done = (f32[1,32,256]{2,1,0:T(8,128)}, f32[1,32,256]{2,1,0:T(8,128)}, f32[1,32,256]{2,1,0:T(8,128)}, f32[1,32,256]{2,1,0:T(8,128)}, ...) async-done(((f32[1,32,256]{2,1,0:T(8,128)}, f32[1,32,256]{2,1,0:T(8,128)}, f32[1,32,256]{2,1,0:T(8,128)}, f32[1,32,256]{2,1,0:T(8,128)}, f32[1,32,256]{2,1,0:T(8,128)}, ...) | async-done | bytes 196624 | tf_op jit(solution)/shard_map/psum | solution.py:37
  234.5 0.8 constant_dynamic-update-slice_fusion.4
  235.3 0.8 constant_dynamic-update-slice_fusion.3
  236.0 0.8 constant_dynamic-update-slice_fusion.2
  237.6 0.8 constant_dynamic-update-slice_fusion
  238.3 57.8 %all-reduce.6.cloned.1.call-done = (f32[32,512]{1,0:T(8,128)}, f32[32,512]{1,0:T(8,128)}, f32[32,512]{1,0:T(8,128)}, f32[32,512]{1,0:T(8,128)}, f32[32,512]{1,0:...) async-done(((f32[32,512]{1,0:T(8,128)}, f32[32,512]{1,0:T(8,128)}, ...) | async-done | bytes 786448 | tf_op jit(solution)/shard_map/psum | solution.py:25
  296.1 0.9 bitcast_dynamic-update-slice_fusion.5
  297.0 0.9 bitcast_dynamic-update-slice_fusion.4
  297.9 0.9 bitcast_dynamic-update-slice_fusion.3
  298.8 0.9 bitcast_dynamic-update-slice_fusion.2
  299.7 0.9 bitcast_dynamic-update-slice_fusion.1
  300.6 0.9 bitcast_dynamic-update-slice_fusion
  301.5 23.2 %reduce-scatter.7.cloned.1.call-done = f32[128,256]{1,0:T(8,128)} async-done(((f32[512,256]{1,0:T(8,128)}), f32[128,256]{1,0:T(8,128)}) %reduce-scatter.7.cloned.1.call-update) | async-done | bytes 131088 | tf_op jit(solution)/shard_map/reduce_scatter | solution.py:40
  324.7 0.9 bitcast_dynamic-update-slice_fusion.11
  325.6 26.9 %reduce-scatter.9.cloned.1.call-done = f32[128,256]{1,0:T(8,128)} async-done(((f32[512,256]{1,0:T(8,128)}), f32[128,256]{1,0:T(8,128)}) %reduce-scatter.9.cloned.1.call-update) | async-done | bytes 131088 | tf_op jit(solution)/shard_map/reduce_scatter | solution.py:40
  352.5 0.9 bitcast_dynamic-update-slice_fusion.10
  353.4 26.9 %reduce-scatter.11.cloned.1.call-done = f32[128,256]{1,0:T(8,128)} async-done(((f32[512,256]{1,0:T(8,128)}), f32[128,256]{1,0:T(8,128)}) %reduce-scatter.11.cloned.1.call-update) | async-done | bytes 131088 | tf_op jit(solution)/shard_map/reduce_scatter | solution.py:40
  380.3 0.9 bitcast_dynamic-update-slice_fusion.9
  381.2 26.9 %reduce-scatter.13.cloned.1.call-done = f32[128,256]{1,0:T(8,128)} async-done(((f32[512,256]{1,0:T(8,128)}), f32[128,256]{1,0:T(8,128)}) %reduce-scatter.13.cloned.1.call-update) | async-done | bytes 131088 | tf_op jit(solution)/shard_map/reduce_scatter | solution.py:40
  408.1 0.9 bitcast_dynamic-update-slice_fusion.8
  409.0 27.0 %reduce-scatter.15.cloned.1.call-done = f32[128,256]{1,0:T(8,128)} async-done(((f32[512,256]{1,0:T(8,128)}), f32[128,256]{1,0:T(8,128)}) %reduce-scatter.15.cloned.1.call-update) | async-done | bytes 131088 | tf_op jit(solution)/shard_map/reduce_scatter | solution.py:40
  436.1 0.9 bitcast_dynamic-update-slice_fusion.7
  437.0 27.0 %reduce-scatter.17.cloned.1.call-done = f32[128,256]{1,0:T(8,128)} async-done(((f32[512,256]{1,0:T(8,128)}), f32[128,256]{1,0:T(8,128)}) %reduce-scatter.17.cloned.1.call-update) | async-done | bytes 131088 | tf_op jit(solution)/shard_map/reduce_scatter | solution.py:40
  464.0 0.9 bitcast_dynamic-update-slice_fusion.6
  (100 shorter events, 7.4 us)
Async XLA Ops:
  7.2 17.5 %copy-start.28 = (bf16[6,128,256]{2,1,0:T(8,128)(2,1)S(1)}, bf16[6,128,256]{2,1,0:T(8,128)(2,1)}, u32[]{:S(2)}) copy-start(bf16[6,128,256]{2,1,0:T(8,128)(2,1)} %param.6) | copy-start | bytes 1179652
  7.2 226.6 %all-reduce.8.cloned.1.call-start = ((), (), s32[]{:S(2)}) async-start(), calls=%async_computation.13 | async-start | bytes 393216 | tf_op jit(solution)/shard_map/psum | solution.py:37
  24.6 31.1 %copy-start.22 = (bf16[1,512,512]{2,1,0:T(8,128)(2,1)}, bf16[1,512,512]{2,1,0:T(8,128)(2,1)S(1)}, u32[]{:S(2)}) copy-start(bf16[1,512,512]{2,1,0:T(8,128)(2,1)S(1)} %all-gather) | copy-start | bytes 1572868
  48.7 8.1 %copy-start.19 = (bf16[1,512,512]{2,1,0:T(8,128)(2,1)}, bf16[1,512,512]{2,1,0:T(8,128)(2,1)S(1)}, u32[]{:S(2)}) copy-start(bf16[1,512,512]{2,1,0:T(8,128)(2,1)S(1)} %all-gather.1) | copy-start | bytes 1572868
  48.7 7.7 %copy-start.25 = (bf16[6,256,512]{2,1,0:T(8,128)(2,1)S(1)}, bf16[6,256,512]{2,1,0:T(8,128)(2,1)}, u32[]{:S(2)}) copy-start(bf16[6,256,512]{2,1,0:T(8,128)(2,1)} %param.8) | copy-start | bytes 4718596
  48.7 7.8 %copy-start.26 = (bf16[6,32,256]{2,1,0:T(8,128)(2,1)S(1)}, bf16[6,32,256]{2,1,0:T(8,128)(2,1)}, u32[]{:S(2)}) copy-start(bf16[6,32,256]{2,1,0:T(8,128)(2,1)} %param.9) | copy-start | bytes 294916
  48.7 7.8 %copy-start.27 = (bf16[6,32,512]{2,1,0:T(8,128)(2,1)S(1)}, bf16[6,32,512]{2,1,0:T(8,128)(2,1)}, u32[]{:S(2)}) copy-start(bf16[6,32,512]{2,1,0:T(8,128)(2,1)} %param.10) | copy-start | bytes 589828
  56.1 1.0 copy-start.2
  56.4 17.5 %copy-start = (f32[256,512]{1,0:T(8,128)}, f32[256,512]{1,0:T(8,128)S(1)}, u32[]{:S(2)}) copy-start(f32[256,512]{1,0:T(8,128)S(1)} %fusion.18) | copy-start | bytes 1572868
  74.0 6.6 %copy-start.23 = (bf16[1,512,512]{2,1,0:T(8,128)(2,1)}, bf16[1,512,512]{2,1,0:T(8,128)(2,1)S(1)}, u32[]{:S(2)}) copy-start(bf16[1,512,512]{2,1,0:T(8,128)(2,1)S(1)} %all-gather.2) | copy-start | bytes 1572868
  80.3 24.6 %copy-start.3 = (f32[256,512]{1,0:T(8,128)}, f32[256,512]{1,0:T(8,128)S(1)}, u32[]{:S(2)}) copy-start(f32[256,512]{1,0:T(8,128)S(1)} %fusion.15) | copy-start | bytes 1572868
  97.6 6.9 %copy-start.20 = (bf16[1,512,512]{2,1,0:T(8,128)(2,1)}, bf16[1,512,512]{2,1,0:T(8,128)(2,1)S(1)}, u32[]{:S(2)}) copy-start(bf16[1,512,512]{2,1,0:T(8,128)(2,1)S(1)} %all-gather.3) | copy-start | bytes 1572868
  104.8 23.2 %copy-start.6 = (f32[256,512]{1,0:T(8,128)}, f32[256,512]{1,0:T(8,128)S(1)}, u32[]{:S(2)}) copy-start(f32[256,512]{1,0:T(8,128)S(1)} %fusion.12) | copy-start | bytes 1572868
  122.0 23.7 %copy-start.17 = (bf16[1,512,512]{2,1,0:T(8,128)(2,1)}, bf16[1,512,512]{2,1,0:T(8,128)(2,1)S(1)}, u32[]{:S(2)}) copy-start(bf16[1,512,512]{2,1,0:T(8,128)(2,1)S(1)} %all-gather.4) | copy-start | bytes 1572868
  128.4 24.4 %copy-start.9 = (f32[256,512]{1,0:T(8,128)}, f32[256,512]{1,0:T(8,128)S(1)}, u32[]{:S(2)}) copy-start(f32[256,512]{1,0:T(8,128)S(1)} %fusion.9) | copy-start | bytes 1572868
  145.7 8.5 %copy-start.15 = (bf16[1,512,512]{2,1,0:T(8,128)(2,1)}, bf16[1,512,512]{2,1,0:T(8,128)(2,1)S(1)}, u32[]{:S(2)}) copy-start(bf16[1,512,512]{2,1,0:T(8,128)(2,1)S(1)} %all-gather.5) | copy-start | bytes 1572868
  145.7 8.5 %copy-start.31 = (f32[6,512]{1,0:T(8,128)S(1)}, f32[6,512]{1,0:T(8,128)}, u32[]{:S(2)}) copy-start(f32[6,512]{1,0:T(8,128)} %param.11) | copy-start | bytes 36868
  153.1 0.8 copy-start.12
  179.4 5.1 %copy-start.4 = (f32[256,512]{1,0:T(8,128)S(1)}, f32[256,512]{1,0:T(8,128)}, u32[]{:S(2)}) copy-start(f32[256,512]{1,0:T(8,128)} %copy-done.3) | copy-start | bytes 1572868
  180.2 5.4 %copy-start.7 = (f32[256,512]{1,0:T(8,128)S(1)}, f32[256,512]{1,0:T(8,128)}, u32[]{:S(2)}) copy-start(f32[256,512]{1,0:T(8,128)} %copy-done.6) | copy-start | bytes 1572868
  182.4 4.3 copy-start.10
  184.5 3.2 copy-start.13
  188.8 107.4 %all-reduce.6.cloned.1.call-start = ((), (), s32[]{:S(2)}) async-start(), calls=%async_computation.12 | async-start | bytes 1572864 | tf_op jit(solution)/shard_map/psum | solution.py:25
  189.0 3.9 copy-start.1
  189.0 5.7 %copy-start.5 = (f32[256,512]{1,0:T(8,128)S(1)}, f32[256,512]{1,0:T(8,128)}, u32[]{:S(2)}) copy-start(f32[256,512]{1,0:T(8,128)} %copy-done.3) | copy-start | bytes 1572868
  191.9 4.6 copy-start.8
  193.8 4.7 copy-start.11
  195.6 4.6 copy-start.14
  201.2 123.5 %reduce-scatter.7.cloned.1.call-start = ((), (), s32[]{:S(2)}) async-start(), calls=%async_computation.6 | async-start | bytes 655360 | tf_op jit(solution)/shard_map/reduce_scatter | solution.py:40
  203.5 2.4 copy-start.24
  203.5 149.0 %reduce-scatter.9.cloned.1.call-start = ((), (), s32[]{:S(2)}) async-start(), calls=%async_computation.7 | async-start | bytes 655360 | tf_op jit(solution)/shard_map/reduce_scatter | solution.py:40
  205.8 1.3 copy-start.21
  205.8 174.5 %reduce-scatter.11.cloned.1.call-start = ((), (), s32[]{:S(2)}) async-start(), calls=%async_computation.8 | async-start | bytes 655360 | tf_op jit(solution)/shard_map/reduce_scatter | solution.py:40
  207.0 1.3 copy-start.18
  207.1 201.1 %reduce-scatter.13.cloned.1.call-start = ((), (), s32[]{:S(2)}) async-start(), calls=%async_computation.9 | async-start | bytes 655360 | tf_op jit(solution)/shard_map/reduce_scatter | solution.py:40
  208.3 1.3 copy-start.16
  208.3 227.8 %reduce-scatter.15.cloned.1.call-start = ((), (), s32[]{:S(2)}) async-start(), calls=%async_computation.10 | async-start | bytes 655360 | tf_op jit(solution)/shard_map/reduce_scatter | solution.py:40
  209.5 254.5 %reduce-scatter.17.cloned.1.call-start = ((), (), s32[]{:S(2)}) async-start(), calls=%async_computation.11 | async-start | bytes 655360 | tf_op jit(solution)/shard_map/reduce_scatter | solution.py:40
  238.3 226.6 %copy-start.32 = (f32[6,32,256]{2,1,0:T(8,128)}, f32[6,32,256]{2,1,0:T(8,128)S(1)}, u32[]{:S(2)}) copy-start(f32[6,32,256]{2,1,0:T(8,128)S(1)} %constant_dynamic-update-slice_fusion) | copy-start | bytes 589828
  301.5 163.5 %copy-start.29 = (f32[6,32,512]{2,1,0:T(8,128)}, f32[6,32,512]{2,1,0:T(8,128)S(1)}, u32[]{:S(2)}) copy-start(f32[6,32,512]{2,1,0:T(8,128)S(1)} %bitcast_dynamic-update-slice_fusion) | copy-start | bytes 1179652
  465.0 0.7 copy-start.30
Sparse Core Ops, SparseCore 0:
  188.9 44.8 all-reduce.7
  237.7 58.3 all-reduce.5
  299.0 25.7 reduce-scatter.6
  327.4 25.0 reduce-scatter.8
  355.2 25.0 reduce-scatter.10
  383.0 25.0 reduce-scatter.12
  410.9 25.0 reduce-scatter.14
  438.9 25.0 reduce-scatter.16
where the time goes:
time: 475 us; the launch traced here: 473 us
  waiting for transfers between devices  238 us (50%)
  blocking collectives  166 us (35%)
  matrix products  33.3 us (7%)
  between operations  14.5 us (3%)
  other arithmetic  11.6 us (2%)
  local copies, waits for them, and re-layouts  7.98 us (2%)
    reduce_scatter x6, waiting for transfers between devices, one_layer(): lax.psum_scatter(lax.dot_general(scaled, weight_low, (((1,), (1,)), ((),...  158 us
    all_gather x6, blocking collectives, one_layer(): grads_all = lax.all_gather(grads, 'row', axis=0, tiled=True)  101 us
    psum x1, waiting for transfers between devices, one_layer(): lax.psum((squares_part, dots_part, inner_outer, inner_merged), 'row')  57.8 us
    all_gather x6, blocking collectives, one_layer(): lax.all_gather(acts, 'col', axis=0, tiled=True)  40.1 us
    psum x1, blocking collectives, one_layer(): lax.psum((squares_part, dots_part, inner_outer, inner_merged), 'row')  25.1 us
    psum x1, waiting for transfers between devices, one_layer(): in_grad = lax.psum(in_part, 'col')  22.4 us
  transfers between devices with their start and end apart: 8, of which 8 were waited for; matrix products, arithmetic and copies ran while one was open for 8% of the time, Pallas kernels for 0%

commit v1 on v0

v1 whole, which is shorter than its diff:
```python
import functools

import jax
import jax.numpy as jnp
from jax import lax
from jax.experimental import pallas as pl
from jax.experimental.pallas import tpu as pltpu
from jax.sharding import PartitionSpec as P

MESH = pl.DeviceIdType.MESH
F32 = jnp.float32
BF16 = jnp.bfloat16


def mm(a, b, dims):
    return lax.dot_general(a, b, (dims, ((), ())), preferred_element_type=F32)


def kernel(
    R, C,
    acts, grads, frozen, ain, aout, mag,
    ig, ing, oug, mgrad,
    G, A, merged, wlow, prod, own, rs_send, rs_recv,
    sq, dt, im_send, im_recv, io_send, io_recv, og, q, q_recv,
    scl, cor, send, g_in, g_fw, a_in, rs_in, sq_in, dt_in, im_in, io_in, og_in, q_in,
):
    L, TR, W = grads.shape
    TC, KI = acts.shape[1:]
    RANK = ain.shape[1]
    k = RANK // R
    Z = R // 2
    r, c = lax.axis_index("row"), lax.axis_index("col")
    z, core = r // 2, lax.rem(r, 2)
    sib = 2 * z + 1 - core

    def row_to(d):
        return lax.rem(r + d, R)

    def row_from(d):
        return lax.rem(r + R - d, R)

    def col_to(d):
        return lax.rem(c + d, C)

    def z_to(d):
        return 2 * lax.rem(z + d, Z) + core

    def z_from(d):
        return 2 * lax.rem(z + Z - d, Z) + core

    def rows(at, size):
        return pl.ds(pl.multiple_of(at * size, size), size)

    def rcopy(src, dst, cat, recv, **dev):
        return pltpu.make_async_remote_copy(
            src_ref=src, dst_ref=dst, send_sem=send.at[cat], recv_sem=recv,
            device_id=dev, device_id_type=MESH,
        )

    barrier = pltpu.get_barrier_semaphore()
    for d in range(1, R):
        pl.semaphore_signal(barrier, inc=1, device_id={"row": row_to(d)}, device_id_type=MESH)
    for d in range(1, C):
        pl.semaphore_signal(barrier, inc=1, device_id={"col": col_to(d)}, device_id_type=MESH)
    pl.semaphore_wait(barrier, R + C - 2)

    def g_copy(l, d):
        peer = sib if d == 0 else z_to(d)
        return rcopy(grads.at[l], G.at[l, rows(r, TR)], 0, g_in.at[l, d], row=peer)

    def a_copy(l, d):
        return rcopy(acts.at[l], A.at[l, rows(c, TC)], 1, a_in.at[l, d], col=col_to(d))

    def fw_copy(l, d):
        block = G.at[l, rows(z_from(d), TR)]
        return rcopy(block, block, 2, g_fw.at[l, d], row=sib)

    def rs_copy(l, d):
        return rcopy(rs_send.at[d, l], rs_recv.at[d, l], 3, rs_in.at[l, d], col=col_to(d))

    def sq_copy(d):
        return rcopy(sq.at[r], sq.at[r], 4, sq_in.at[d], row=row_to(d))

    def dt_copy(d):
        return rcopy(dt.at[r], dt.at[r], 5, dt_in.at[d], row=row_to(d))

    def im_copy(d):
        return rcopy(im_send.at[row_to(d)], im_recv.at[r], 6, im_in.at[d], row=row_to(d))

    def io_copy(d):
        return rcopy(io_send.at[row_to(d)], io_recv.at[r], 7, io_in.at[d], row=row_to(d))

    def og_copy(d):
        return rcopy(og.at[r], og.at[r], 8, og_in.at[d], row=row_to(d))

    def q_copy(d):
        return rcopy(q, q_recv.at[d], 9, q_in.at[d], col=col_to(d))

    @pl.loop(0, L)
    def _(l):
        for d in range(Z):
            g_copy(l, d).start()
        for d in range(1, C):
            a_copy(l, d).start()

    @pl.loop(0, L)
    def _(l):
        G[l, rows(r, TR)] = grads[l]
        A[l, rows(c, TC)] = acts[l]
        m = frozen[l].astype(F32) + mm(ain[l], aout[l], ((0,), (0,)))
        merged[l] = m
        low = m.astype(BF16)
        wlow[l] = low
        sq[r, l] = jnp.sum(m * m, axis=0, keepdims=True)
        inner = mm(ain[l], low, ((1,), (0,)))
        for s in range(R):
            im_send[s, l] = inner[s * k:(s + 1) * k]

    for d in range(1, R):
        sq_copy(d).start()
    for d in range(1, R):
        im_copy(d).start()
    im_recv[r] = im_send[r]
    for d in range(1, R):
        rcopy(sq.at[r], sq.at[row_from(d)], 4, sq_in.at[d], row=r).wait_recv()
    total = sq[0]
    for s in range(1, R):
        total = total + sq[s]
    scl[...] = mag[...] / jnp.sqrt(total + 0.25)

    @pl.loop(0, L)
    def _(l):
        for d in range(1, Z):
            rcopy(grads.at[l], G.at[l, rows(z_from(d), TR)], 0, g_in.at[l, d], row=r).wait_recv()
            fw_copy(l, d).start()
        rcopy(grads.at[l], G.at[l, rows(sib, TR)], 0, g_in.at[l, 0], row=r).wait_recv()
        for d in range(1, Z):
            from_sib = 2 * lax.rem(z + Z - d, Z) + 1 - core
            rcopy(grads.at[l], G.at[l, rows(from_sib, TR)], 2, g_fw.at[l, d], row=r).wait_recv()
        scale = scl[l]
        g = G[l]
        scaled = (g.astype(F32) * scale).astype(BF16)
        prod[...] = mm(scaled, wlow[l], ((1,), (1,)))
        for d in range(1, C):
            rs_send[d, l] = prod[rows(col_to(d), TC)].astype(BF16)
            rs_copy(l, d).start()
        own[l] = prod[rows(c, TC)]
        for d in range(1, C):
            src = lax.rem(c + C - d, C)
            rcopy(acts.at[l], A.at[l, rows(src, TC)], 1, a_in.at[l, d], col=c).wait_recv()
        outer = mm(A[l], g, ((0,), (0,)))
        dt[r, l] = jnp.sum(merged[l] * outer, axis=0, keepdims=True)
        inner = mm(ain[l], outer.astype(BF16), ((1,), (0,)))
        for s in range(R):
            io_send[s, l] = inner[s * k:(s + 1) * k]
        ing[l] = mm(aout[l], (outer * scale).astype(BF16), ((1,), (1,)))

    for d in range(1, R):
        dt_copy(d).start()
    for d in range(1, R):
        io_copy(d).start()
    io_recv[r] = io_send[r]
    for d in range(1, R):
        rcopy(dt.at[r], dt.at[row_from(d)], 5, dt_in.at[d], row=r).wait_recv()
    dots = dt[0]
    for s in range(1, R):
        dots = dots + dt[s]
    norms = jnp.sqrt(total + 0.25)
    mgrad[...] = dots / norms
    cor[...] = -mag[...] * dots / (norms * norms * norms)

    @pl.loop(0, L)
    def _(l):
        adjusted = (merged[l] * cor[l]).astype(BF16)
        part = ing[l] + mm(aout[l], adjusted, ((1,), (1,)))
        ing[l] = part
        q[l] = part.astype(BF16)

    for d in range(1, C):
        q_copy(d).start()
    for d in range(1, R):
        rcopy(im_recv.at[r], im_recv.at[row_from(d)], 6, im_in.at[d], row=r).wait_recv()
        rcopy(io_recv.at[r], io_recv.at[row_from(d)], 7, io_in.at[d], row=r).wait_recv()

    @pl.loop(0, L)
    def _(l):
        summed, side = io_recv[0, l], im_recv[0, l]
        for s in range(1, R):
            summed = summed + io_recv[s, l]
            side = side + im_recv[s, l]
        og[r, l] = summed * scl[l] + side * cor[l]

    for d in range(1, R):
        og_copy(d).start()

    @pl.loop(0, L)
    def _(l):
        result = own[l]
        for d in range(1, C):
            rcopy(rs_send.at[d, l], rs_recv.at[d, l], 3, rs_in.at[l, d], col=c).wait_recv()
            result = result + rs_recv[d, l].astype(F32)
        ig[l] = result.astype(BF16)

    for d in range(1, C):
        rcopy(q, q_recv.at[d], 9, q_in.at[d], col=c).wait_recv()

    @pl.loop(0, L)
    def _(l):
        result = ing[l]
        for d in range(1, C):
            result = result + q_recv[d, l].astype(F32)
        ing[l] = result

    for d in range(1, R):
        rcopy(og.at[r], og.at[row_from(d)], 8, og_in.at[d], row=r).wait_recv()

    @pl.loop(0, L)
    def _(l):
        for s in range(R):
            oug[l, s * k:(s + 1) * k] = og[s, l]

    @pl.loop(0, L)
    def _(l):
        for d in range(Z):
            g_copy(l, d).wait_send()
        for d in range(1, Z):
            fw_copy(l, d).wait_send()
        for d in range(1, C):
            a_copy(l, d).wait_send()
            rs_copy(l, d).wait_send()

    for d in range(1, R):
        sq_copy(d).wait_send()
        im_copy(d).wait_send()
        dt_copy(d).wait_send()
        io_copy(d).wait_send()
        og_copy(d).wait_send()
    for d in range(1, C):
        q_copy(d).wait_send()


def body(R, C, acts, grads, frozen, ain, aout, mag):
    L, TR, W = grads.shape
    TC, KI = acts.shape[1:]
    RANK = ain.shape[1]
    k, T, Z = RANK // R, TR * R, R // 2
    V = pltpu.VMEM
    dma = pltpu.SemaphoreType.DMA
    vm = pl.BlockSpec(memory_space=pltpu.VMEM)
    ig, ing, oug, mgrad = pl.pallas_call(
        functools.partial(kernel, R, C),
        out_shape=(
            jax.ShapeDtypeStruct((L, TC, KI), BF16),
            jax.ShapeDtypeStruct((L, RANK, KI), F32),
            jax.ShapeDtypeStruct((L, RANK, W), F32),
            jax.ShapeDtypeStruct((L, 1, W), F32),
        ),
        in_specs=[vm] * 6,
        out_specs=(vm,) * 4,
        scratch_shapes=[
            V((L, T, W), BF16), V((L, T, KI), BF16), V((L, KI, W), F32), V((L, KI, W), BF16),
            V((T, KI), F32), V((L, TC, KI), F32), V((C, L, TC, KI), BF16), V((C, L, TC, KI), BF16),
            V((R, L, 1, W), F32), V((R, L, 1, W), F32),
            V((R, L, k, W), F32), V((R, L, k, W), F32), V((R, L, k, W), F32), V((R, L, k, W), F32),
            V((R, L, k, W), F32), V((L, RANK, KI), BF16), V((C, L, RANK, KI), BF16),
            V((L, 1, W), F32), V((L, 1, W), F32),
            dma((10,)), dma((L, Z)), dma((L, Z)), dma((L, C)), dma((L, C)),
            dma((R,)), dma((R,)), dma((R,)), dma((R,)), dma((R,)), dma((C,)),
        ],
        compiler_params=pltpu.CompilerParams(
            collective_id=0, has_side_effects=True, vmem_limit_bytes=60 * 1024 * 1024
        ),
    )(acts, grads, frozen, ain, aout, mag[:, None, :])
    return ig, ing, oug, mgrad[:, 0, :]


def solution(mesh):
    return jax.shard_map(
        functools.partial(body, mesh.shape["row"], mesh.shape["col"]),
        mesh=mesh,
        in_specs=(
            P(None, "col", "row"),
            P(None, "row", "col"),
            P(None, "row", "col"),
            P(None, None, "row"),
            P(None, None, "col"),
            P(None, "col"),
        ),
        out_specs=(
            P(None, "col", "row"),
            P(None, None, "row"),
            P(None, None, "col"),
            P(None, "col"),
        ),
        check_vma=False,
    )
```

time: 475 us -> 93.5 us (0.20)
  waiting for transfers between devices: 238 us -> 0 us
  blocking collectives: 166 us -> 0 us
  Pallas kernels: 0 us -> 83.4 us
  matrix products: 33.3 us -> 0 us
  between operations: 14.5 us -> 0.64 us
  other arithmetic: 11.6 us -> 0 us
    reduce_scatter x6 -> x0, waiting for transfers between devices: 158 us -> none  [one_layer(): lax.psum_scatter(lax.dot_general(scaled, weight_low, (((1,), (1,)), ((),...]
    all_gather x12 -> x0, blocking collectives: 141 us -> none  [the longest x6 101 us: one_layer(): grads_all = lax.all_gather(grads, 'row', axis=0, tiled=True)]
    pallas_call x0 -> x1, Pallas kernels: none -> 83.4 us  [body(): pl.pallas_call(functools.partial(kernel, R, C), out_shape=(jax.ShapeDtype...]
    psum x2 -> x0, waiting for transfers between devices: 80.2 us -> none  [the longest x1 57.8 us: one_layer(): lax.psum((squares_part, dots_part, inner_outer, inner_merged), 'row')]
    dot_general x36 -> x0, matrix products: 33.3 us -> none  [the longest x6 8.99 us: one_layer(): lax.dot_general(scaled, weight_low, (((1,), (1,)), ((), ())), preferred_e...]
    psum x1 -> x0, blocking collectives: 25.1 us -> none  [one_layer(): lax.psum((squares_part, dots_part, inner_outer, inner_merged), 'row')]
    unnamed x10 -> x0, other arithmetic: 8.99 us -> none
  transfers between devices with their start and end apart: 8 -> 0, of which waited for: 8 -> 0; matrix products, arithmetic and copies ran while one was open for 8% -> 0% of each run, Pallas kernels for 0% -> 0%
where the time goes in v1:
time: 93.5 us; the launch traced here: 91.8 us
  Pallas kernels  83.4 us (89%)
  local copies, waits for them, and re-layouts  7.8 us (8%)
    pallas_call x1, Pallas kernels, body(): pl.pallas_call(functools.partial(kernel, R, C), out_shape=(jax.ShapeDtype...  83.4 us
    unnamed x4, local copies, waits for them, and re-layouts  6.47 us

profile of v1, /device:TPU:1, one launch (start us, length us, event | category | flops | bytes accessed | tf_op | source)
XLA Modules:
  0.0 91.8 jit_solution(14616661980353366969)
XLA Ops:
  0.6 1.3 %broadcast_in_dim.3.mag = f32[6,1,512]{2,1,0:T(1,128)} reshape(f32[6,512]{1,0:T(8,128)} %param.11) | data formatting | bytes 24576 | tf_op jit(solution)/shard_map/broadcast_in_dim | solution.py:273
  2.0 83.4 %shard_map.93 = (bf16[6,128,256]{2,1,0:T(8,128)(2,1)}, f32[6,32,256]{2,1,0:T(8,128)}, f32[6,32,512]{2,1,0:T(8,128)}, f32[6,1,512]{2,1,0:T(1,128)}) custom-call(bf16[6,128,256]{2,1,0:T(8,128)(2,1)} %acts.1, bf16[6,64,512]{2,1,0:T(8,128)(2,1)} %grads.1, bf16[6,256,512]{2,1,0:T(8,128)(2,1)} %frozen.1, bf16[6,32,256]{2,1,0:T(8,128)(2,1)} %ain.1, ...), custom_call_target="tpu_custom_call" | custom-call | tf_op jit(solution)/shard_map/pallas_call | solution.py:250
  85.3 1.3 %copy.12 = f32[6,1,512]{2,0,1:T(8,128)} copy(f32[6,1,512]{2,1,0:T(1,128)} %get-tuple-element.11) | data formatting | bytes 24576
  86.7 1.8 %copy.16 = bf16[6,128,256]{2,1,0:T(8,128)(2,1)} copy(bf16[6,128,256]{2,1,0:T(8,128)(2,1)} %get-tuple-element.16) | data formatting | bytes 786432
  88.4 1.6 %copy.17 = f32[6,32,256]{2,1,0:T(8,128)} copy(f32[6,32,256]{2,1,0:T(8,128)} %get-tuple-element.17) | data formatting | bytes 393216
  90.0 1.8 %copy.18 = f32[6,32,512]{2,1,0:T(8,128)} copy(f32[6,32,512]{2,1,0:T(8,128)} %get-tuple-element.18) | data formatting | bytes 786432

commit v2 on v1

--- a/solution.py
+++ b/solution.py
@@ -21,8 +21,8 @@
     acts, grads, frozen, ain, aout, mag,
     ig, ing, oug, mgrad,
     G, A, merged, wlow, prod, own, rs_send, rs_recv,
-    sq, dt, im_send, im_recv, io_send, io_recv, og, q, q_recv,
-    scl, cor, send, g_in, g_fw, a_in, rs_in, sq_in, dt_in, im_in, io_in, og_in, q_in,
+    sq, dt, im_send, im_sib, im_acc, im_recv, io_send, io_sib, io_acc, io_recv, og, q, q_recv,
+    scl, cor, mag3, send, g_in, g_fw, a_in, rs_in, sq_in, dt_in, im_in, io_in, io_fw, og_in, og_fw, q_in,
 ):
     L, TR, W = grads.shape
     TC, KI = acts.shape[1:]
@@ -81,20 +81,31 @@
     def sq_copy(d):
         return rcopy(sq.at[r], sq.at[r], 4, sq_in.at[d], row=row_to(d))
 
-    def dt_copy(d):
-        return rcopy(dt.at[r], dt.at[r], 5, dt_in.at[d], row=row_to(d))
+    def dt_copy(l, d):
+        return rcopy(dt.at[r, l], dt.at[r, l], 5, dt_in.at[l, d], row=row_to(d))
+
+    def at_z(d):
+        return lax.rem(z + d, Z)
 
     def im_copy(d):
-        return rcopy(im_send.at[row_to(d)], im_recv.at[r], 6, im_in.at[d], row=row_to(d))
-
-    def io_copy(d):
-        return rcopy(io_send.at[row_to(d)], io_recv.at[r], 7, io_in.at[d], row=row_to(d))
+        if d == 0:
+            return rcopy(im_send.at[1 - core], im_sib, 6, im_in.at[0], row=sib)
+        return rcopy(im_acc.at[at_z(d)], im_recv.at[z], 7, im_in.at[d], row=z_to(d))
+
+    def io_fw_copy(l):
+        return rcopy(io_send.at[1 - core, l], io_sib.at[l], 8, io_fw.at[l], row=sib)
+
+    def io_copy(l, d):
+        return rcopy(io_acc.at[at_z(d), l], io_recv.at[z, l], 9, io_in.at[l, d], row=z_to(d))
 
     def og_copy(d):
-        return rcopy(og.at[r], og.at[r], 8, og_in.at[d], row=row_to(d))
+        return rcopy(og.at[r], og.at[r], 11, og_in.at[d], row=sib if d == 0 else z_to(d))
+
+    def og_fw_copy(d):
+        return rcopy(og.at[z_from(d)], og.at[z_from(d)], 12, og_fw.at[d], row=sib)
 
     def q_copy(d):
-        return rcopy(q, q_recv.at[d], 9, q_in.at[d], col=col_to(d))
+        return rcopy(q, q_recv.at[d], 10, q_in.at[d], col=col_to(d))
 
     @pl.loop(0, L)
     def _(l):
@@ -114,19 +125,32 @@
         sq[r, l] = jnp.sum(m * m, axis=0, keepdims=True)
         inner = mm(ain[l], low, ((1,), (0,)))
         for s in range(R):
-            im_send[s, l] = inner[s * k:(s + 1) * k]
+            im_send[s % 2, s // 2, l] = inner[s * k:(s + 1) * k]
 
     for d in range(1, R):
         sq_copy(d).start()
-    for d in range(1, R):
-        im_copy(d).start()
-    im_recv[r] = im_send[r]
+    im_copy(0).start()
+    for l in range(L):
+        mag3[l] = mag[l:l + 1]
     for d in range(1, R):
         rcopy(sq.at[r], sq.at[row_from(d)], 4, sq_in.at[d], row=r).wait_recv()
     total = sq[0]
     for s in range(1, R):
         total = total + sq[s]
-    scl[...] = mag[...] / jnp.sqrt(total + 0.25)
+    scl[...] = mag3[...] / jnp.sqrt(total + 0.25)
+    im_copy(0).wait_recv()
+    im_acc[...] = im_send[core] + im_sib[...]
+    for d in range(1, Z):
+        im_copy(d).start()
+    im_recv[z] = im_acc[z]
+
+    def pass_on(l):
+        rcopy(io_sib.at[l], io_sib.at[l], 8, io_fw.at[l], row=sib).wait_recv()
+        for s in range(Z):
+            io_acc[s, l] = io_send[core, l, s] + io_sib[l, s]
+        for d in range(1, Z):
+            io_copy(l, d).start()
+        io_recv[z, l] = io_acc[z, l]
 
     @pl.loop(0, L)
     def _(l):
@@ -150,24 +174,34 @@
             rcopy(acts.at[l], A.at[l, rows(src, TC)], 1, a_in.at[l, d], col=c).wait_recv()
         outer = mm(A[l], g, ((0,), (0,)))
         dt[r, l] = jnp.sum(merged[l] * outer, axis=0, keepdims=True)
+        for d in range(1, R):
+            dt_copy(l, d).start()
         inner = mm(ain[l], outer.astype(BF16), ((1,), (0,)))
         for s in range(R):
-            io_send[s, l] = inner[s * k:(s + 1) * k]
+            io_send[s % 2, l, s // 2] = inner[s * k:(s + 1) * k]
+        io_fw_copy(l).start()
+
+        @pl.when(l > 0)
+        def _():
+            pass_on(l - 1)
+
         ing[l] = mm(aout[l], (outer * scale).astype(BF16), ((1,), (1,)))
 
-    for d in range(1, R):
-        dt_copy(d).start()
-    for d in range(1, R):
-        io_copy(d).start()
-    io_recv[r] = io_send[r]
-    for d in range(1, R):
-        rcopy(dt.at[r], dt.at[row_from(d)], 5, dt_in.at[d], row=r).wait_recv()
+    pass_on(L - 1)
+
+    @pl.loop(0, L)
+    def _(l):
+        for d in range(1, R):
+            rcopy(dt.at[r, l], dt.at[row_from(d), l], 5, dt_in.at[l, d], row=r).wait_recv()
+
     dots = dt[0]
     for s in range(1, R):
         dots = dots + dt[s]
     norms = jnp.sqrt(total + 0.25)
-    mgrad[...] = dots / norms
-    cor[...] = -mag[...] * dots / (norms * norms * norms)
+    ratio = dots / norms
+    for l in range(L):
+        mgrad[l:l + 1] = ratio[l]
+    cor[...] = -mag3[...] * dots / (norms * norms * norms)
 
     @pl.loop(0, L)
     def _(l):
@@ -178,19 +212,22 @@
 
     for d in range(1, C):
         q_copy(d).start()
-    for d in range(1, R):
-        rcopy(im_recv.at[r], im_recv.at[row_from(d)], 6, im_in.at[d], row=r).wait_recv()
-        rcopy(io_recv.at[r], io_recv.at[row_from(d)], 7, io_in.at[d], row=r).wait_recv()
-
-    @pl.loop(0, L)
-    def _(l):
+    for d in range(1, Z):
+        src = lax.rem(z + Z - d, Z)
+        rcopy(im_recv.at[z], im_recv.at[src], 7, im_in.at[d], row=r).wait_recv()
+
+    @pl.loop(0, L)
+    def _(l):
+        for d in range(1, Z):
+            src = lax.rem(z + Z - d, Z)
+            rcopy(io_recv.at[z, l], io_recv.at[src, l], 9, io_in.at[l, d], row=r).wait_recv()
         summed, side = io_recv[0, l], im_recv[0, l]
-        for s in range(1, R):
+        for s in range(1, Z):
             summed = summed + io_recv[s, l]
             side = side + im_recv[s, l]
         og[r, l] = summed * scl[l] + side * cor[l]
 
-    for d in range(1, R):
+    for d in range(Z):
         og_copy(d).start()
 
     @pl.loop(0, L)
@@ -202,7 +239,7 @@
         ig[l] = result.astype(BF16)
 
     for d in range(1, C):
-        rcopy(q, q_recv.at[d], 9, q_in.at[d], col=c).wait_recv()
+        rcopy(q, q_recv.at[d], 10, q_in.at[d], col=c).wait_recv()
 
     @pl.loop(0, L)
     def _(l):
@@ -211,8 +248,13 @@
             result = result + q_recv[d, l].astype(F32)
         ing[l] = result
 
-    for d in range(1, R):
-        rcopy(og.at[r], og.at[row_from(d)], 8, og_in.at[d], row=r).wait_recv()
+    for d in range(1, Z):
+        rcopy(og.at[r], og.at[z_from(d)], 11, og_in.at[d], row=r).wait_recv()
+        og_fw_copy(d).start()
+    rcopy(og.at[r], og.at[sib], 11, og_in.at[0], row=r).wait_recv()
+    for d in range(1, Z):
+        from_sib = 2 * lax.rem(z + Z - d, Z) + 1 - core
+        rcopy(og.at[r], og.at[from_sib], 12, og_fw.at[d], row=r).wait_recv()
 
     @pl.loop(0, L)
     def _(l):
@@ -229,14 +271,30 @@
             a_copy(l, d).wait_send()
             rs_copy(l, d).wait_send()
 
+    @pl.loop(0, L)
+    def _(l):
+        for d in range(1, R):
+            dt_copy(l, d).wait_send()
+        io_fw_copy(l).wait_send()
+        for d in range(1, Z):
+            io_copy(l, d).wait_send()
+
     for d in range(1, R):
         sq_copy(d).wait_send()
+    for d in range(Z):
         im_copy(d).wait_send()
-        dt_copy(d).wait_send()
-        io_copy(d).wait_send()
         og_copy(d).wait_send()
+    for d in range(1, Z):
+        og_fw_copy(d).wait_send()
     for d in range(1, C):
         q_copy(d).wait_send()
+
+
+def finish(ig, ing, oug, mgrad, ig_out, ing_out, oug_out, mgrad_out):
+    ig_out[...] = ig[...]
+    ing_out[...] = ing[...]
+    oug_out[...] = oug[...]
+    mgrad_out[...] = mgrad[...]
 
 
 def body(R, C, acts, grads, frozen, ain, aout, mag):
@@ -253,7 +311,7 @@
             jax.ShapeDtypeStruct((L, TC, KI), BF16),
             jax.ShapeDtypeStruct((L, RANK, KI), F32),
             jax.ShapeDtypeStruct((L, RANK, W), F32),
-            jax.ShapeDtypeStruct((L, 1, W), F32),
+            jax.ShapeDtypeStruct((L, W), F32),
         ),
         in_specs=[vm] * 6,
         out_specs=(vm,) * 4,
@@ -261,17 +319,23 @@
             V((L, T, W), BF16), V((L, T, KI), BF16), V((L, KI, W), F32), V((L, KI, W), BF16),
             V((T, KI), F32), V((L, TC, KI), F32), V((C, L, TC, KI), BF16), V((C, L, TC, KI), BF16),
             V((R, L, 1, W), F32), V((R, L, 1, W), F32),
-            V((R, L, k, W), F32), V((R, L, k, W), F32), V((R, L, k, W), F32), V((R, L, k, W), F32),
+            V((2, Z, L, k, W), F32), V((Z, L, k, W), F32), V((Z, L, k, W), F32), V((Z, L, k, W), F32),
+            V((2, L, Z, k, W), F32), V((L, Z, k, W), F32), V((Z, L, k, W), F32), V((Z, L, k, W), F32),
             V((R, L, k, W), F32), V((L, RANK, KI), BF16), V((C, L, RANK, KI), BF16),
-            V((L, 1, W), F32), V((L, 1, W), F32),
-            dma((10,)), dma((L, Z)), dma((L, Z)), dma((L, C)), dma((L, C)),
-            dma((R,)), dma((R,)), dma((R,)), dma((R,)), dma((R,)), dma((C,)),
+            V((L, 1, W), F32), V((L, 1, W), F32), V((L, 1, W), F32),
+            dma((13,)), dma((L, Z)), dma((L, Z)), dma((L, C)), dma((L, C)),
+            dma((R,)), dma((L, R)), dma((Z,)), dma((L, Z)), dma((L,)), dma((Z,)), dma((Z,)), dma((C,)),
         ],
         compiler_params=pltpu.CompilerParams(
-            collective_id=0, has_side_effects=True, vmem_limit_bytes=60 * 1024 * 1024
+            collective_id=0, has_side_effects=True, vmem_limit_bytes=44 * 1024 * 1024
         ),
-    )(acts, grads, frozen, ain, aout, mag[:, None, :])
-    return ig, ing, oug, mgrad[:, 0, :]
+    )(acts, grads, frozen, ain, aout, mag)
+    return pl.pallas_call(
+        finish,
+        out_shape=tuple(jax.ShapeDtypeStruct(x.shape, x.dtype) for x in (ig, ing, oug, mgrad)),
+        in_specs=[vm] * 4,
+        out_specs=(vm,) * 4,
+    )(ig, ing, oug, mgrad)
 
 
 def solution(mesh):

time: 93.5 us -> 84.4 us (0.903); the launches traced: 91.8 us -> 84 us
  Pallas kernels: 83.4 us -> 74.7 us
    pallas_call x1, Pallas kernels: 83.4 us -> 72.5 us  [body(): pl.pallas_call(functools.partial(kernel, R, C), out_shape=(jax.ShapeDtype...]
    unnamed x4 -> x20, local copies, waits for them, and re-layouts: 6.47 us -> 8.68 us
    pallas_call x0 -> x1, Pallas kernels: none -> 2.18 us  [body(): pl.pallas_call(finish, out_shape=tuple((jax.ShapeDtypeStruct(x.shape, x.d...]
    broadcast_in_dim x1 -> x0, local copies, waits for them, and re-layouts: 1.33 us -> none  [body(): mag[:, None, :]]
where the time goes in v2:
time: 84.4 us; the launch traced here: 84 us
  Pallas kernels  74.7 us (89%)
  local copies, waits for them, and re-layouts  8.68 us (10%)
    pallas_call x1, Pallas kernels, body(): pl.pallas_call(functools.partial(kernel, R, C), out_shape=(jax.ShapeDtype...  72.5 us
    unnamed x20, local copies, waits for them, and re-layouts  8.68 us
    pallas_call x1, Pallas kernels, body(): pl.pallas_call(finish, out_shape=tuple((jax.ShapeDtypeStruct(x.shape, x.d...  2.18 us

profile of v2, /device:TPU:1, one launch (start us, length us, event | category | flops | bytes accessed | tf_op | source)
XLA Modules:
  0.0 84.0 jit_solution(954519169510496770)
XLA Ops:
  0.6 0.0 copy-start
  0.6 1.4 %copy-done = bf16[6,256,512]{2,1,0:T(8,128)(2,1)S(1)} copy-done((bf16[6,256,512]{2,1,0:T(8,128)(2,1)S(1)}, bf16[6,256,512]{2,1,0:T(8,128)(2,1)}, u32[]{:S(2)}) %copy-start) | copy-done | bytes 1572888
  2.0 0.0 copy-start.3
  2.0 1.0 %copy-done.3 = bf16[6,128,256]{2,1,0:T(8,128)(2,1)S(1)} copy-done((bf16[6,128,256]{2,1,0:T(8,128)(2,1)S(1)}, bf16[6,128,256]{2,1,0:T(8,128)(2,1)}, u32[]{:S(2)}) %copy-start.3) | copy-done | bytes 393240
  3.0 0.0 copy-start.4
  3.0 1.0 %copy-done.4 = bf16[6,64,512]{2,1,0:T(8,128)(2,1)S(1)} copy-done((bf16[6,64,512]{2,1,0:T(8,128)(2,1)S(1)}, bf16[6,64,512]{2,1,0:T(8,128)(2,1)}, u32[]{:S(2)}) %copy-start.4) | copy-done | bytes 393240
  4.0 0.0 copy-start.6
  4.0 0.9 %copy-done.6 = bf16[6,32,512]{2,1,0:T(8,128)(2,1)S(1)} copy-done((bf16[6,32,512]{2,1,0:T(8,128)(2,1)S(1)}, bf16[6,32,512]{2,1,0:T(8,128)(2,1)}, u32[]{:S(2)}) %copy-start.6) | copy-done | bytes 196632
  5.0 0.0 copy-start.7
  5.0 0.9 %copy-done.7 = bf16[6,32,256]{2,1,0:T(8,128)(2,1)S(1)} copy-done((bf16[6,32,256]{2,1,0:T(8,128)(2,1)S(1)}, bf16[6,32,256]{2,1,0:T(8,128)(2,1)}, u32[]{:S(2)}) %copy-start.7) | copy-done | bytes 98328
  5.9 0.0 copy-start.8
  5.9 0.7 copy-done.8
  6.6 72.5 %shard_map.93 = (bf16[6,128,256]{2,1,0:T(8,128)(2,1)S(1)}, f32[6,32,256]{2,1,0:T(8,128)S(1)}, f32[6,32,512]{2,1,0:T(8,128)S(1)}, f32[6,512]{1,0:T(8,128)S(1)}) custom-call(bf16[6,128,256]{2,1,0:T(8,128)(2,1)S(1)} %copy-done.3, bf16[6,64,512]{2,1,0:T(8,128)(2,1)S(1)} %copy-done.4, bf16[6,256,512]{2,1,0:T(8,128)(2,1)S(1)} %copy-done, ...), custom_call_target="tpu_custom_call" | custom-call | tf_op jit(solution)/shard_map/pallas_call | solution.py:308
  79.1 0.0 copy-start.1
  79.1 0.7 copy-done.1
  79.8 0.0 copy-start.2
  79.9 0.7 copy-done.2
  80.6 0.0 copy-start.5
  80.6 0.7 copy-done.5
  81.3 0.0 copy-start.9
  81.3 0.6 copy-done.9
  81.9 2.2 %shard_map.94 = (bf16[6,128,256]{2,1,0:T(8,128)(2,1)}, f32[6,32,256]{2,1,0:T(8,128)}, f32[6,32,512]{2,1,0:T(8,128)}, f32[6,512]{1,0:T(8,128)}) custom-call(bf16[6,128,256]{2,1,0:T(8,128)(2,1)} %copy-done.1, f32[6,32,256]{2,1,0:T(8,128)} %copy-done.5, f32[6,32,512]{2,1,0:T(8,128)} %copy-done.2, f32[6,512]{1,0:T(8,128)} %copy-done.9), custom_call_target="tpu_custom_call" | custom-call | tf_op jit(solution)/shard_map/pallas_call | solution.py:333
Async XLA Ops:
  0.6 1.4 %copy-start = (bf16[6,256,512]{2,1,0:T(8,128)(2,1)S(1)}, bf16[6,256,512]{2,1,0:T(8,128)(2,1)}, u32[]{:S(2)}) copy-start(bf16[6,256,512]{2,1,0:T(8,128)(2,1)} %frozen.1) | copy-start | bytes 4718596
  2.0 1.0 %copy-start.3 = (bf16[6,128,256]{2,1,0:T(8,128)(2,1)S(1)}, bf16[6,128,256]{2,1,0:T(8,128)(2,1)}, u32[]{:S(2)}) copy-start(bf16[6,128,256]{2,1,0:T(8,128)(2,1)} %acts.1) | copy-start | bytes 1179652
  3.0 1.0 %copy-start.4 = (bf16[6,64,512]{2,1,0:T(8,128)(2,1)S(1)}, bf16[6,64,512]{2,1,0:T(8,128)(2,1)}, u32[]{:S(2)}) copy-start(bf16[6,64,512]{2,1,0:T(8,128)(2,1)} %grads.1) | copy-start | bytes 1179652
  4.0 0.9 %copy-start.6 = (bf16[6,32,512]{2,1,0:T(8,128)(2,1)S(1)}, bf16[6,32,512]{2,1,0:T(8,128)(2,1)}, u32[]{:S(2)}) copy-start(bf16[6,32,512]{2,1,0:T(8,128)(2,1)} %aout.1) | copy-start | bytes 589828
  5.0 0.9 %copy-start.7 = (bf16[6,32,256]{2,1,0:T(8,128)(2,1)S(1)}, bf16[6,32,256]{2,1,0:T(8,128)(2,1)}, u32[]{:S(2)}) copy-start(bf16[6,32,256]{2,1,0:T(8,128)(2,1)} %ain.1) | copy-start | bytes 294916
  5.9 0.7 copy-start.8
  79.1 0.7 copy-start.1
  79.8 0.7 copy-start.2
  80.6 0.7 copy-start.5
  81.3 0.6 copy-start.9

commit v3 on v2

--- a/solution.py
+++ b/solution.py
@@ -18,17 +18,27 @@
 
 def kernel(
     R, C,
+    acts_hbm, grads_hbm, frozen_hbm, ain_hbm, aout_hbm, mag_hbm,
+    ig_hbm, ing_hbm, oug_hbm, mgrad_hbm,
     acts, grads, frozen, ain, aout, mag,
-    ig, ing, oug, mgrad,
+    ig, ing, oug, mgrad, load, save,
     G, A, merged, wlow, prod, own, rs_send, rs_recv,
     sq, dt, im_send, im_sib, im_acc, im_recv, io_send, io_sib, io_acc, io_recv, og, q, q_recv,
     scl, cor, mag3, send, g_in, g_fw, a_in, rs_in, sq_in, dt_in, im_in, io_in, io_fw, og_in, og_fw, q_in,
 ):
+    pairs = ((grads_hbm, grads), (acts_hbm, acts), (frozen_hbm, frozen),
+             (ain_hbm, ain), (aout_hbm, aout), (mag_hbm, mag))
+    loads = [pltpu.make_async_copy(a, b, load.at[i]) for i, (a, b) in enumerate(pairs)]
+    for copy in loads:
+        copy.start()
+    pairs = ((mgrad, mgrad_hbm), (ig, ig_hbm), (ing, ing_hbm), (oug, oug_hbm))
+    saves = [pltpu.make_async_copy(a, b, save.at[i]) for i, (a, b) in enumerate(pairs)]
     L, TR, W = grads.shape
     TC, KI = acts.shape[1:]
     RANK = ain.shape[1]
     k = RANK // R
     Z = R // 2
+    ahead = min(4, L)
     r, c = lax.axis_index("row"), lax.axis_index("col")
     z, core = r // 2, lax.rem(r, 2)
     sib = 2 * z + 1 - core
@@ -64,16 +74,48 @@
         pl.semaphore_signal(barrier, inc=1, device_id={"col": col_to(d)}, device_id_type=MESH)
     pl.semaphore_wait(barrier, R + C - 2)
 
-    def g_copy(l, d):
-        peer = sib if d == 0 else z_to(d)
-        return rcopy(grads.at[l], G.at[l, rows(r, TR)], 0, g_in.at[l, d], row=peer)
+    def g_block(l, at, which):
+        return G.at[l, rows(2 * at + which, TR)]
+
+    def g_own(l, step):
+        if step == 0:
+            return rcopy(grads.at[l], g_block(l, z, core), 2, g_fw.at[l, z], row=sib)
+        return rcopy(grads.at[l], g_block(l, z, core), 0, g_in.at[l, z], row=r + 2 * step)
+
+    def g_pass(l, at, step):
+        block = g_block(l, at, core)
+        if step == 0:
+            return rcopy(block, block, 2, g_fw.at[l, at], row=sib)
+        return rcopy(block, block, 0, g_in.at[l, at], row=r + 2 * step)
+
+    def g_own_each(l, act):
+        act(g_own(l, 0))
+
+        @pl.when(z < Z - 1)
+        def _():
+            act(g_own(l, 1))
+
+        @pl.when(z > 0)
+        def _():
+            act(g_own(l, -1))
+
+    def g_relay(l, d, act, arrive):
+        for step in (1, -1):
+            at = z - step * d
+
+            @pl.when(jnp.logical_and(at >= 0, at < Z))
+            def _():
+                if arrive:
+                    rcopy(grads.at[l], g_block(l, at, core), 0, g_in.at[l, at], row=r).wait_recv()
+
+                @pl.when(jnp.logical_and(z + step >= 0, z + step < Z))
+                def _():
+                    act(g_pass(l, at, step))
+
+                act(g_pass(l, at, 0))
 
     def a_copy(l, d):
         return rcopy(acts.at[l], A.at[l, rows(c, TC)], 1, a_in.at[l, d], col=col_to(d))
-
-    def fw_copy(l, d):
-        block = G.at[l, rows(z_from(d), TR)]
-        return rcopy(block, block, 2, g_fw.at[l, d], row=sib)
 
     def rs_copy(l, d):
         return rcopy(rs_send.at[d, l], rs_recv.at[d, l], 3, rs_in.at[l, d], col=col_to(d))
@@ -107,12 +149,20 @@
     def q_copy(d):
         return rcopy(q, q_recv.at[d], 10, q_in.at[d], col=col_to(d))
 
-    @pl.loop(0, L)
-    def _(l):
-        for d in range(Z):
-            g_copy(l, d).start()
+    loads[0].wait()
+    loads[1].wait()
+
+    @pl.loop(0, L)
+    def _(l):
+        @pl.when(l < ahead)
+        def _():
+            g_own_each(l, lambda copy: copy.start())
+
         for d in range(1, C):
             a_copy(l, d).start()
+
+    for copy in loads[2:]:
+        copy.wait()
 
     @pl.loop(0, L)
     def _(l):
@@ -138,12 +188,6 @@
     for s in range(1, R):
         total = total + sq[s]
     scl[...] = mag3[...] / jnp.sqrt(total + 0.25)
-    im_copy(0).wait_recv()
-    im_acc[...] = im_send[core] + im_sib[...]
-    for d in range(1, Z):
-        im_copy(d).start()
-    im_recv[z] = im_acc[z]
-
     def pass_on(l):
         rcopy(io_sib.at[l], io_sib.at[l], 8, io_fw.at[l], row=sib).wait_recv()
         for s in range(Z):
@@ -152,15 +196,9 @@
             io_copy(l, d).start()
         io_recv[z, l] = io_acc[z, l]
 
-    @pl.loop(0, L)
-    def _(l):
-        for d in range(1, Z):
-            rcopy(grads.at[l], G.at[l, rows(z_from(d), TR)], 0, g_in.at[l, d], row=r).wait_recv()
-            fw_copy(l, d).start()
-        rcopy(grads.at[l], G.at[l, rows(sib, TR)], 0, g_in.at[l, 0], row=r).wait_recv()
-        for d in range(1, Z):
-            from_sib = 2 * lax.rem(z + Z - d, Z) + 1 - core
-            rcopy(grads.at[l], G.at[l, rows(from_sib, TR)], 2, g_fw.at[l, d], row=r).wait_recv()
+    def compute(l):
+        for at in range(Z):
+            rcopy(grads.at[l], g_block(l, at, 1 - core), 2, g_fw.at[l, at], row=r).wait_recv()
         scale = scl[l]
         g = G[l]
         scaled = (g.astype(F32) * scale).astype(BF16)
@@ -187,6 +225,31 @@
 
         ing[l] = mm(aout[l], (outer * scale).astype(BF16), ((1,), (1,)))
 
+    @pl.loop(0, L + Z - 1)
+    def _(at):
+        @pl.when(at + ahead < L)
+        def _():
+            g_own_each(at + ahead, lambda copy: copy.start())
+
+        for d in range(1, Z):
+            l = at - (d - 1)
+
+            @pl.when(jnp.logical_and(l >= 0, l < L))
+            def _():
+                g_relay(l, d, lambda copy: copy.start(), True)
+
+        @pl.when(at == L - 1)
+        def _():
+            im_copy(0).wait_recv()
+            im_acc[...] = im_send[core] + im_sib[...]
+            for d in range(1, Z):
+                im_copy(d).start()
+            im_recv[z] = im_acc[z]
+
+        @pl.when(at >= Z - 1)
+        def _():
+            compute(at - (Z - 1))
+
     pass_on(L - 1)
 
     @pl.loop(0, L)
@@ -201,6 +264,7 @@
     ratio = dots / norms
     for l in range(L):
         mgrad[l:l + 1] = ratio[l]
+    saves[0].start()
     cor[...] = -mag3[...] * dots / (norms * norms * norms)
 
     @pl.loop(0, L)
@@ -238,6 +302,8 @@
             result = result + rs_recv[d, l].astype(F32)
         ig[l] = result.astype(BF16)
 
+    saves[1].start()
+
     for d in range(1, C):
         rcopy(q, q_recv.at[d], 10, q_in.at[d], col=c).wait_recv()
 
@@ -247,6 +313,8 @@
         for d in range(1, C):
             result = result + q_recv[d, l].astype(F32)
         ing[l] = result
+
+    saves[2].start()
 
     for d in range(1, Z):
         rcopy(og.at[r], og.at[z_from(d)], 11, og_in.at[d], row=r).wait_recv()
@@ -261,12 +329,13 @@
         for s in range(R):
             oug[l, s * k:(s + 1) * k] = og[s, l]
 
-    @pl.loop(0, L)
-    def _(l):
-        for d in range(Z):
-            g_copy(l, d).wait_send()
+    saves[3].start()
+
+    @pl.loop(0, L)
+    def _(l):
+        g_own_each(l, lambda copy: copy.wait_send())
         for d in range(1, Z):
-            fw_copy(l, d).wait_send()
+            g_relay(l, d, lambda copy: copy.wait_send(), False)
         for d in range(1, C):
             a_copy(l, d).wait_send()
             rs_copy(l, d).wait_send()
@@ -288,6 +357,8 @@
         og_fw_copy(d).wait_send()
     for d in range(1, C):
         q_copy(d).wait_send()
+    for copy in saves:
+        copy.wait()
 
 
 def finish(ig, ing, oug, mgrad, ig_out, ing_out, oug_out, mgrad_out):
@@ -305,6 +376,7 @@
     V = pltpu.VMEM
     dma = pltpu.SemaphoreType.DMA
     vm = pl.BlockSpec(memory_space=pltpu.VMEM)
+    hbm = pl.BlockSpec(memory_space=pltpu.HBM)
     ig, ing, oug, mgrad = pl.pallas_call(
         functools.partial(kernel, R, C),
         out_shape=(
@@ -313,9 +385,13 @@
             jax.ShapeDtypeStruct((L, RANK, W), F32),
             jax.ShapeDtypeStruct((L, W), F32),
         ),
-        in_specs=[vm] * 6,
-        out_specs=(vm,) * 4,
+        in_specs=[hbm] * 6,
+        out_specs=(hbm,) * 4,
         scratch_shapes=[
+            V(acts.shape, BF16), V(grads.shape, BF16), V(frozen.shape, BF16),
+            V(ain.shape, BF16), V(aout.shape, BF16), V(mag.shape, F32),
+            V((L, TC, KI), BF16), V((L, RANK, KI), F32), V((L, RANK, W), F32), V((L, W), F32),
+            dma((6,)), dma((4,)),
             V((L, T, W), BF16), V((L, T, KI), BF16), V((L, KI, W), F32), V((L, KI, W), BF16),
             V((T, KI), F32), V((L, TC, KI), F32), V((C, L, TC, KI), BF16), V((C, L, TC, KI), BF16),
             V((R, L, 1, W), F32), V((R, L, 1, W), F32),
@@ -327,7 +403,7 @@
             dma((R,)), dma((L, R)), dma((Z,)), dma((L, Z)), dma((L,)), dma((Z,)), dma((Z,)), dma((C,)),
         ],
         compiler_params=pltpu.CompilerParams(
-            collective_id=0, has_side_effects=True, vmem_limit_bytes=44 * 1024 * 1024
+            collective_id=0, has_side_effects=True, vmem_limit_bytes=60 * 1024 * 1024
         ),
     )(acts, grads, frozen, ain, aout, mag)
     return pl.pallas_call(

time: 84.4 us -> 63.3 us (0.75)
  Pallas kernels: 74.7 us -> 62.5 us
  local copies, waits for them, and re-layouts: 8.68 us -> 0 us
    pallas_call x1, Pallas kernels: 72.5 us -> 60.3 us  [body(): pl.pallas_call(functools.partial(kernel, R, C), out_shape=(jax.ShapeDtype...]
    unnamed x20 -> x0, local copies, waits for them, and re-layouts: 8.68 us -> none
where the time goes in v3:
time: 63.3 us; the launch traced here: 63.1 us
  Pallas kernels  62.5 us (99%)
  between operations  0.64 us (1%)
    pallas_call x1, Pallas kernels, body(): pl.pallas_call(functools.partial(kernel, R, C), out_shape=(jax.ShapeDtype...  60.3 us
    pallas_call x1, Pallas kernels, body(): pl.pallas_call(finish, out_shape=tuple((jax.ShapeDtypeStruct(x.shape, x.d...  2.18 us

profile of v3, /device:TPU:1, one launch (start us, length us, event | category | flops | bytes accessed | tf_op | source)
XLA Modules:
  0.0 63.1 jit_solution(10613482258925861099)
XLA Ops:
  0.6 60.3 %shard_map.93 = (bf16[6,128,256]{2,1,0:T(8,128)(2,1)}, f32[6,32,256]{2,1,0:T(8,128)}, f32[6,32,512]{2,1,0:T(8,128)}, f32[6,512]{1,0:T(8,128)}) custom-call(bf16[6,128,256]{2,1,0:T(8,128)(2,1)} %acts_hbm.1, bf16[6,64,512]{2,1,0:T(8,128)(2,1)} %grads_hbm.1, bf16[6,256,512]{2,1,0:T(8,128)(2,1)} %frozen_hbm.1, bf16[6,32,256]{2,1,0:T(8,128)(2,1)} %ain_hbm.1, ...), custom_call_target="tpu_custom_call" | custom-call | tf_op jit(solution)/shard_map/pallas_call | solution.py:380
  60.9 2.2 %shard_map.94 = (bf16[6,128,256]{2,1,0:T(8,128)(2,1)}, f32[6,32,256]{2,1,0:T(8,128)}, f32[6,32,512]{2,1,0:T(8,128)}, f32[6,512]{1,0:T(8,128)}) custom-call(bf16[6,128,256]{2,1,0:T(8,128)(2,1)} %get-tuple-element.8.ig, f32[6,32,256]{2,1,0:T(8,128)} %get-tuple-element.9.ing, f32[6,32,512]{2,1,0:T(8,128)} %get-tuple-element.10.oug, ...), custom_call_target="tpu_custom_call" | custom-call | tf_op jit(solution)/shard_map/pallas_call | solution.py:409

commit v4 on v3

--- a/solution.py
+++ b/solution.py
@@ -38,7 +38,8 @@
     RANK = ain.shape[1]
     k = RANK // R
     Z = R // 2
-    ahead = min(4, L)
+    ahead = min(3, L)
+    skew = (Z - 2) // 2
     r, c = lax.axis_index("row"), lax.axis_index("col")
     z, core = r // 2, lax.rem(r, 2)
     sib = 2 * z + 1 - core
@@ -91,13 +92,10 @@
     def g_own_each(l, act):
         act(g_own(l, 0))
 
-        @pl.when(z < Z - 1)
-        def _():
-            act(g_own(l, 1))
-
-        @pl.when(z > 0)
-        def _():
-            act(g_own(l, -1))
+        for step in (1, -1, 2, -2):
+            @pl.when(jnp.logical_and(z + step >= 0, z + step < Z))
+            def _():
+                act(g_own(l, step))
 
     def g_relay(l, d, act, arrive):
         for step in (1, -1):
@@ -108,9 +106,10 @@
                 if arrive:
                     rcopy(grads.at[l], g_block(l, at, core), 0, g_in.at[l, at], row=r).wait_recv()
 
-                @pl.when(jnp.logical_and(z + step >= 0, z + step < Z))
-                def _():
-                    act(g_pass(l, at, step))
+                for far in (2 * step, step) if d % 2 == 0 else ():
+                    @pl.when(jnp.logical_and(z + far >= 0, z + far < Z))
+                    def _():
+                        act(g_pass(l, at, far))
 
                 act(g_pass(l, at, 0))
 
@@ -180,6 +179,8 @@
     for d in range(1, R):
         sq_copy(d).start()
     im_copy(0).start()
+    if ahead < L:
+        g_own_each(ahead, lambda copy: copy.start())
     for l in range(L):
         mag3[l] = mag[l:l + 1]
     for d in range(1, R):
@@ -225,14 +226,14 @@
 
         ing[l] = mm(aout[l], (outer * scale).astype(BF16), ((1,), (1,)))
 
-    @pl.loop(0, L + Z - 1)
+    @pl.loop(0, L + skew)
     def _(at):
-        @pl.when(at + ahead < L)
+        @pl.when(at + ahead + 1 < L)
         def _():
-            g_own_each(at + ahead, lambda copy: copy.start())
+            g_own_each(at + ahead + 1, lambda copy: copy.start())
 
         for d in range(1, Z):
-            l = at - (d - 1)
+            l = at - (d - 1) // 2
 
             @pl.when(jnp.logical_and(l >= 0, l < L))
             def _():
@@ -246,9 +247,9 @@
                 im_copy(d).start()
             im_recv[z] = im_acc[z]
 
-        @pl.when(at >= Z - 1)
+        @pl.when(at >= skew)
         def _():
-            compute(at - (Z - 1))
+            compute(at - skew)
 
     pass_on(L - 1)
 

time: 63.3 us -> 65.4 us (1.033)
  Pallas kernels: 62.5 us -> 64.6 us
    pallas_call x1, Pallas kernels: 60.3 us -> 62.4 us  [body(): pl.pallas_call(functools.partial(kernel, R, C), out_shape=(jax.ShapeDtype...]
where the time goes in v4:
time: 65.4 us; the launch traced here: 65.3 us
  Pallas kernels  64.6 us (99%)
    pallas_call x1, Pallas kernels, body(): pl.pallas_call(functools.partial(kernel, R, C), out_shape=(jax.ShapeDtype...  62.4 us
    pallas_call x1, Pallas kernels, body(): pl.pallas_call(finish, out_shape=tuple((jax.ShapeDtypeStruct(x.shape, x.d...  2.18 us

profile of v4, /device:TPU:1, one launch (start us, length us, event | category | flops | bytes accessed | tf_op | source)
XLA Modules:
  0.0 65.3 jit_solution(5979022218387240025)
XLA Ops:
  0.6 62.4 %shard_map.93 = (bf16[6,128,256]{2,1,0:T(8,128)(2,1)}, f32[6,32,256]{2,1,0:T(8,128)}, f32[6,32,512]{2,1,0:T(8,128)}, f32[6,512]{1,0:T(8,128)}) custom-call(bf16[6,128,256]{2,1,0:T(8,128)(2,1)} %acts_hbm.1, bf16[6,64,512]{2,1,0:T(8,128)(2,1)} %grads_hbm.1, bf16[6,256,512]{2,1,0:T(8,128)(2,1)} %frozen_hbm.1, bf16[6,32,256]{2,1,0:T(8,128)(2,1)} %ain_hbm.1, ...), custom_call_target="tpu_custom_call" | custom-call | tf_op jit(solution)/shard_map/pallas_call | solution.py:381
  63.1 2.2 %shard_map.94 = (bf16[6,128,256]{2,1,0:T(8,128)(2,1)}, f32[6,32,256]{2,1,0:T(8,128)}, f32[6,32,512]{2,1,0:T(8,128)}, f32[6,512]{1,0:T(8,128)}) custom-call(bf16[6,128,256]{2,1,0:T(8,128)(2,1)} %get-tuple-element.8.ig, f32[6,32,256]{2,1,0:T(8,128)} %get-tuple-element.9.ing, f32[6,32,512]{2,1,0:T(8,128)} %get-tuple-element.10.oug, ...), custom_call_target="tpu_custom_call" | custom-call | tf_op jit(solution)/shard_map/pallas_call | solution.py:410

commit v5 on v3

--- a/solution.py
+++ b/solution.py
@@ -182,12 +182,19 @@
     im_copy(0).start()
     for l in range(L):
         mag3[l] = mag[l:l + 1]
-    for d in range(1, R):
-        rcopy(sq.at[r], sq.at[row_from(d)], 4, sq_in.at[d], row=r).wait_recv()
-    total = sq[0]
-    for s in range(1, R):
-        total = total + sq[s]
-    scl[...] = mag3[...] / jnp.sqrt(total + 0.25)
+    if ahead < L:
+        g_own_each(ahead, lambda copy: copy.start())
+
+    def scales_ready():
+        for d in range(1, R):
+            rcopy(sq.at[r], sq.at[row_from(d)], 4, sq_in.at[d], row=r).wait_recv()
+        total = sq[0]
+        for s in range(1, R):
+            total = total + sq[s]
+        norms = jnp.sqrt(total + 0.25)
+        cor[...] = norms
+        scl[...] = mag3[...] / norms
+
     def pass_on(l):
         rcopy(io_sib.at[l], io_sib.at[l], 8, io_fw.at[l], row=sib).wait_recv()
         for s in range(Z):
@@ -227,9 +234,9 @@
 
     @pl.loop(0, L + Z - 1)
     def _(at):
-        @pl.when(at + ahead < L)
-        def _():
-            g_own_each(at + ahead, lambda copy: copy.start())
+        @pl.when(at + ahead + 1 < L)
+        def _():
+            g_own_each(at + ahead + 1, lambda copy: copy.start())
 
         for d in range(1, Z):
             l = at - (d - 1)
@@ -238,7 +245,7 @@
             def _():
                 g_relay(l, d, lambda copy: copy.start(), True)
 
-        @pl.when(at == L - 1)
+        @pl.when(at == L + Z - 3)
         def _():
             im_copy(0).wait_recv()
             im_acc[...] = im_send[core] + im_sib[...]
@@ -246,6 +253,10 @@
                 im_copy(d).start()
             im_recv[z] = im_acc[z]
 
+        @pl.when(at == Z - 1)
+        def _():
+            scales_ready()
+
         @pl.when(at >= Z - 1)
         def _():
             compute(at - (Z - 1))
@@ -260,7 +271,7 @@
     dots = dt[0]
     for s in range(1, R):
         dots = dots + dt[s]
-    norms = jnp.sqrt(total + 0.25)
+    norms = cor[...]
     ratio = dots / norms
     for l in range(L):
         mgrad[l:l + 1] = ratio[l]

time: 63.3 us -> 60.5 us (0.956)
  Pallas kernels: 62.5 us -> 59.7 us
    pallas_call x1, Pallas kernels: 60.3 us -> 57.5 us  [body(): pl.pallas_call(functools.partial(kernel, R, C), out_shape=(jax.ShapeDtype...]
where the time goes in v5:
time: 60.5 us; the launch traced here: 60.3 us
  Pallas kernels  59.7 us (99%)
  between operations  0.64 us (1%)
    pallas_call x1, Pallas kernels, body(): pl.pallas_call(functools.partial(kernel, R, C), out_shape=(jax.ShapeDtype...  57.5 us
    pallas_call x1, Pallas kernels, body(): pl.pallas_call(finish, out_shape=tuple((jax.ShapeDtypeStruct(x.shape, x.d...  2.18 us

profile of v5, /device:TPU:1, one launch (start us, length us, event | category | flops | bytes accessed | tf_op | source)
XLA Modules:
  0.0 60.3 jit_solution(10132741241369352336)
XLA Ops:
  0.6 57.5 %shard_map.93 = (bf16[6,128,256]{2,1,0:T(8,128)(2,1)}, f32[6,32,256]{2,1,0:T(8,128)}, f32[6,32,512]{2,1,0:T(8,128)}, f32[6,512]{1,0:T(8,128)}) custom-call(bf16[6,128,256]{2,1,0:T(8,128)(2,1)} %acts_hbm.1, bf16[6,64,512]{2,1,0:T(8,128)(2,1)} %grads_hbm.1, bf16[6,256,512]{2,1,0:T(8,128)(2,1)} %frozen_hbm.1, bf16[6,32,256]{2,1,0:T(8,128)(2,1)} %ain_hbm.1, ...), custom_call_target="tpu_custom_call" | custom-call | tf_op jit(solution)/shard_map/pallas_call | solution.py:391
  58.2 2.2 %shard_map.94 = (bf16[6,128,256]{2,1,0:T(8,128)(2,1)}, f32[6,32,256]{2,1,0:T(8,128)}, f32[6,32,512]{2,1,0:T(8,128)}, f32[6,512]{1,0:T(8,128)}) custom-call(bf16[6,128,256]{2,1,0:T(8,128)(2,1)} %get-tuple-element.8.ig, f32[6,32,256]{2,1,0:T(8,128)} %get-tuple-element.9.ing, f32[6,32,512]{2,1,0:T(8,128)} %get-tuple-element.10.oug, ...), custom_call_target="tpu_custom_call" | custom-call | tf_op jit(solution)/shard_map/pallas_call | solution.py:420

commit v6 on v5

--- a/solution.py
+++ b/solution.py
@@ -232,7 +232,7 @@
 
         ing[l] = mm(aout[l], (outer * scale).astype(BF16), ((1,), (1,)))
 
-    @pl.loop(0, L + Z - 1)
+    @pl.loop(0, L + Z - 2)
     def _(at):
         @pl.when(at + ahead + 1 < L)
         def _():
@@ -253,13 +253,13 @@
                 im_copy(d).start()
             im_recv[z] = im_acc[z]
 
-        @pl.when(at == Z - 1)
+        @pl.when(at == Z - 2)
         def _():
             scales_ready()
 
-        @pl.when(at >= Z - 1)
-        def _():
-            compute(at - (Z - 1))
+        @pl.when(at >= Z - 2)
+        def _():
+            compute(at - (Z - 2))
 
     pass_on(L - 1)
 

time: 60.5 us -> 61 us (level)
  no operation moved by 1% of the time
where the time goes in v6:
time: 61 us; the launch traced here: 60.9 us
  Pallas kernels  60.2 us (99%)
  between operations  0.64 us (1%)
    pallas_call x1, Pallas kernels, body(): pl.pallas_call(functools.partial(kernel, R, C), out_shape=(jax.ShapeDtype...  58.1 us
    pallas_call x1, Pallas kernels, body(): pl.pallas_call(finish, out_shape=tuple((jax.ShapeDtypeStruct(x.shape, x.d...  2.18 us

profile of v6, /device:TPU:1, one launch (start us, length us, event | category | flops | bytes accessed | tf_op | source)
XLA Modules:
  0.0 60.9 jit_solution(1608159738416304117)
XLA Ops:
  0.6 58.1 %shard_map.93 = (bf16[6,128,256]{2,1,0:T(8,128)(2,1)}, f32[6,32,256]{2,1,0:T(8,128)}, f32[6,32,512]{2,1,0:T(8,128)}, f32[6,512]{1,0:T(8,128)}) custom-call(bf16[6,128,256]{2,1,0:T(8,128)(2,1)} %acts_hbm.1, bf16[6,64,512]{2,1,0:T(8,128)(2,1)} %grads_hbm.1, bf16[6,256,512]{2,1,0:T(8,128)(2,1)} %frozen_hbm.1, bf16[6,32,256]{2,1,0:T(8,128)(2,1)} %ain_hbm.1, ...), custom_call_target="tpu_custom_call" | custom-call | tf_op jit(solution)/shard_map/pallas_call | solution.py:391
  58.7 2.2 %shard_map.94 = (bf16[6,128,256]{2,1,0:T(8,128)(2,1)}, f32[6,32,256]{2,1,0:T(8,128)}, f32[6,32,512]{2,1,0:T(8,128)}, f32[6,512]{1,0:T(8,128)}) custom-call(bf16[6,128,256]{2,1,0:T(8,128)(2,1)} %get-tuple-element.8.ig, f32[6,32,256]{2,1,0:T(8,128)} %get-tuple-element.9.ing, f32[6,32,512]{2,1,0:T(8,128)} %get-tuple-element.10.oug, ...), custom_call_target="tpu_custom_call" | custom-call | tf_op jit(solution)/shard_map/pallas_call | solution.py:420
